TPU v7x, 32 devices: a whole 2x2x4 slice. The times are simulated.
32 devices in a mesh: win: 4 (over z), slab: 8 (over y, x, core).
Axes of the slice: x: 2, y: 2, z: 4, core: 2. Of those that a mesh axis runs over, the one named last changes fastest.
Arguments:
- lambdas: float32 [16], P('win'), parts along dimension 0, may hold values from 0 to 1
- charge_a: float32 [16, 4096], P('win', 'slab'), parts along dimension 0, may hold values from -3 to 3
- charge_b: float32 [16, 4096], P('win', 'slab'), parts along dimension 0, may hold values from -3 to 3
- perturbed: int32 [16, 4096], P('win', 'slab'), parts along dimension 0, may hold values 0 or 1
- grid_index: int32 [3, 16, 4096], P(None, 'win', 'slab'), parts along dimension 1, may hold values from 0 to 127, as said below
- spline_weights: float32 [3, 4, 16, 4096], P(None, None, 'win', 'slab'), parts along dimension 2, may hold values from 0 to 1, as said below
- spline_slopes: float32 [3, 4, 16, 4096], P(None, None, 'win', 'slab'), parts along dimension 2, may hold values from -1 to 1, as said below
Outputs:
- forces: float32 [3, 16, 4096], P(None, 'win', 'slab'), parts along dimension 1
- energy: float32 [16], P('win'), parts along dimension 0
- lambda_slope: float32 [16], P('win'), parts along dimension 0
There are 4 independent parts, one for each index of `win`. A program takes and returns all parts, laid end to end along the dimension named above; each array names one. Nothing has to cross between parts.
Inputs may be any that keep to these rules, and one draw needn't show every extreme that they name: `grid_index`: the z index of atom i lies in the planes of the slab index that holds it: from (i // 512) * 16 to that plus 16 - 1. `spline_weights`: along each dimension the four weights are the cubic B-spline values (1-u)^3/6, (3u^3-6u^2+4)/6, (-3u^3+3u^2+3u+1)/6, u^3/6 of the atom's fractional offset u in [0, 1). `spline_slopes`: the derivatives in u of spline_weights at the same offsets.
All inputs are finite; a program needn't handle non-finite values. No bound on the sum of `perturbed` on one device may be relied on, other than what follows from the above.
Results may differ from a plain program's by a relative error of at most 0.0003.
Values sent between devices are 32-bit elements; how exact they have to be, the bound alone decides.
A program may use at most 64 MiB of HBM per device.

v0:
```python
import math

import jax
import jax.numpy as jnp
from jax import lax
from jax.sharding import PartitionSpec as P

NX = 128
NY = 128
NZ = 128


highest = lax.Precision.HIGHEST
gauss_width = 2.0


def passed_along(value, axis, steps):
    count = lax.axis_size(axis)
    pairs = [(source, (source + steps) % count) for source in range(count)]
    return lax.ppermute(value, axis, pairs)


def dft_tables(length):
    counter = jnp.arange(length, dtype=jnp.int32)
    product = counter[:, None] * counter[None, :] % length
    angles = product.astype(jnp.float32) * (2.0 * math.pi / length)
    return (jnp.cos(angles), jnp.sin(angles))


def frequency(counter, length):
    return jnp.where(counter >= length // 2, counter - length, counter).astype(jnp.float32) / length


def stencil_table(first_cell, weights, length):
    grid_cells = jnp.arange(length, dtype=jnp.int32)
    matrix = jnp.zeros((first_cell.shape[0], length), jnp.float32)
    for offset in range(4):
        target = (first_cell + offset) % length
        matrix = matrix + weights[offset][:, None] * (
            grid_cells[None, :] == target[:, None]
        ).astype(jnp.float32)
    return matrix


def plane_table(first_cell, weights, plane_count):
    planes = jnp.arange(plane_count, dtype=jnp.int32)
    matrix = jnp.zeros((plane_count, first_cell.shape[0]), jnp.float32)
    for offset in range(4):
        matrix = matrix + weights[offset][None, :] * (
            planes[:, None] == (first_cell + offset)[None, :]
        ).astype(jnp.float32)
    return matrix


def spread_block(charge, cell_index, weights, first_plane, plane_count):
    rows_x = stencil_table(cell_index[0], weights[0], NX)
    rows_y = stencil_table(cell_index[1], weights[1], NY)
    depth_table = plane_table(cell_index[2] - first_plane, weights[2], plane_count)
    right_side = (depth_table * charge[None, :]).T[:, :, None] * rows_y[:, None, :]
    return jnp.einsum("ia,ipb->pab", rows_x, right_side, precision=highest)


def sample_block(
    charge, charge_step, cell_index, weights, slopes, values, first_plane, plane_count
):
    rows_x = stencil_table(cell_index[0], weights[0], NX)
    steep_x = stencil_table(cell_index[0], slopes[0], NX)
    rows_y = stencil_table(cell_index[1], weights[1], NY)
    steep_y = stencil_table(cell_index[1], slopes[1], NY)
    depth_table = plane_table(cell_index[2] - first_plane, weights[2], plane_count)
    steep_z = plane_table(cell_index[2] - first_plane, slopes[2], plane_count)
    along_rows = jnp.einsum("pab,ib->ipa", values, rows_y, precision=highest)
    reduced = jnp.einsum("ia,ipa->ip", rows_x, along_rows, precision=highest)
    reduced_dx = jnp.einsum("ia,ipa->ip", steep_x, along_rows, precision=highest)
    along_steep = jnp.einsum("pab,ib->ipa", values, steep_y, precision=highest)
    reduced_dy = jnp.einsum("ia,ipa->ip", rows_x, along_steep, precision=highest)
    sampled = jnp.einsum("pi,ip->i", depth_table, reduced, precision=highest)
    force_x = -charge * jnp.einsum("pi,ip->i", depth_table, reduced_dx, precision=highest)
    force_y = -charge * jnp.einsum("pi,ip->i", depth_table, reduced_dy, precision=highest)
    force_z = -charge * jnp.einsum("pi,ip->i", steep_z, reduced, precision=highest)
    return (jnp.stack([force_x, force_y, force_z]), jnp.sum(charge_step * sampled))


def xy_forward(owned_grid, planar):
    cosine_x, sine_x, cosine_y, sine_y = planar
    part_real = jnp.einsum("ka,wpab->wpkb", cosine_x, owned_grid, precision=highest)
    part_imaginary = -jnp.einsum("ka,wpab->wpkb", sine_x, owned_grid, precision=highest)
    plane_real = jnp.einsum("wpkb,bl->wpkl", part_real, cosine_y, precision=highest) + jnp.einsum(
        "wpkb,bl->wpkl", part_imaginary, sine_y, precision=highest
    )
    plane_imaginary = jnp.einsum(
        "wpkb,bl->wpkl", part_imaginary, cosine_y, precision=highest
    ) - jnp.einsum("wpkb,bl->wpkl", part_real, sine_y, precision=highest)
    return jnp.stack([plane_real, plane_imaginary], axis=1)


def xy_inverse(slab_values, planar):
    cosine_x, sine_x, cosine_y, sine_y = planar
    value_real = slab_values[:, 0]
    value_imaginary = slab_values[:, 1]
    half_real = jnp.einsum("wpkl,lb->wpkb", value_real, cosine_y, precision=highest) - jnp.einsum(
        "wpkl,lb->wpkb", value_imaginary, sine_y, precision=highest
    )
    half_imaginary = jnp.einsum(
        "wpkl,lb->wpkb", value_imaginary, cosine_y, precision=highest
    ) + jnp.einsum("wpkl,lb->wpkb", value_real, sine_y, precision=highest)
    return jnp.einsum("ak,wpkb->wpab", cosine_x, half_real, precision=highest) - jnp.einsum(
        "ak,wpkb->wpab", sine_x, half_imaginary, precision=highest
    )


def influence_block(first_column, column_count):
    freq_z = frequency(jnp.arange(NZ, dtype=jnp.int32), NZ)[:, None, None]
    freq_x = frequency(first_column + jnp.arange(column_count, dtype=jnp.int32), NX)[None, :, None]
    freq_y = frequency(jnp.arange(NY, dtype=jnp.int32), NY)[None, None, :]
    squared = freq_z * freq_z + freq_x * freq_x + freq_y * freq_y
    positive = squared > 0
    safe_value = jnp.where(positive, squared, jnp.float32(1.0))
    return jnp.where(
        positive,
        jnp.exp(-gauss_width * squared) / (math.pi * NX * NY * NZ * safe_value),
        jnp.float32(0.0),
    )


def column_transform(columns, influence, cosine_z, sine_z):
    column_real = columns[:, 0]
    column_imaginary = columns[:, 1]
    depth_real = jnp.einsum("kz,nzab->nkab", cosine_z, column_real, precision=highest) + jnp.einsum(
        "kz,nzab->nkab", sine_z, column_imaginary, precision=highest
    )
    depth_imaginary = jnp.einsum(
        "kz,nzab->nkab", cosine_z, column_imaginary, precision=highest
    ) - jnp.einsum("kz,nzab->nkab", sine_z, column_real, precision=highest)
    energy_part = 0.5 * jnp.sum(
        influence * (depth_real * depth_real + depth_imaginary * depth_imaginary), axis=(1, 2, 3)
    )
    scaled_real = influence * depth_real
    scaled_imaginary = influence * depth_imaginary
    back_real = jnp.einsum("zk,nkab->nzab", cosine_z, scaled_real, precision=highest) - jnp.einsum(
        "zk,nkab->nzab", sine_z, scaled_imaginary, precision=highest
    )
    back_imaginary = jnp.einsum(
        "zk,nkab->nzab", cosine_z, scaled_imaginary, precision=highest
    ) + jnp.einsum("zk,nkab->nzab", sine_z, scaled_real, precision=highest)
    return (jnp.stack([back_real, back_imaginary], axis=1), energy_part)


def body(lambdas, charge_a, charge_b, perturbed, grid_index, spline_weights, spline_slopes):
    atoms_here = charge_a.shape[1]
    slab_count = lax.axis_size("slab")
    slab_depth = NZ // slab_count
    flag_values = perturbed.astype(jnp.float32)
    charges = charge_a + flag_values * lambdas[:, None] * (charge_b - charge_a)
    charge_steps = flag_values * (charge_b - charge_a)
    weight_windows = jnp.moveaxis(spline_weights, 2, 0)
    slope_windows = jnp.moveaxis(spline_slopes, 2, 0)
    index_windows = jnp.moveaxis(grid_index, 1, 0)
    cosine_x, sine_x = dft_tables(NX)
    cosine_y, sine_y = dft_tables(NY)
    cosine_z, sine_z = dft_tables(NZ)
    planar = (cosine_x, sine_x, cosine_y, sine_y)
    plane_count = slab_depth + 3
    column_count = NX // slab_count
    first_plane = lax.axis_index("slab") * slab_depth

    def spread_window(inputs):
        return spread_block(inputs[0], inputs[1], inputs[2], first_plane, plane_count)

    extended = lax.map(spread_window, (charges, index_windows, weight_windows))
    reach_count = (slab_depth + 2) // slab_depth
    owned_grid = extended[:, :slab_depth]
    for distance in range(1, reach_count + 1):
        last_plane = min(plane_count, (distance + 1) * slab_depth)
        arrived = passed_along(extended[:, distance * slab_depth : last_plane], "slab", distance)
        owned_grid = owned_grid + jnp.pad(
            arrived, ((0, 0), (0, slab_depth - arrived.shape[1]), (0, 0), (0, 0))
        )
    slab_spectrum = xy_forward(owned_grid, planar)
    influence = influence_block(lax.axis_index("slab") * column_count, column_count)
    stacked, energy_part = column_transform(
        lax.all_to_all(slab_spectrum, "slab", split_axis=3, concat_axis=2, tiled=True),
        influence,
        cosine_z,
        sine_z,
    )
    slab_values = lax.all_to_all(stacked, "slab", split_axis=2, concat_axis=3, tiled=True)
    slab_values, energy_part = (slab_values, energy_part)
    potential = xy_inverse(slab_values, planar)
    pieces = [potential]
    for distance in range(1, reach_count + 1):
        depth_taken = min(slab_depth, plane_count - distance * slab_depth)
        pieces.append(passed_along(potential[:, :depth_taken], "slab", -distance))
    potential_field = jnp.concatenate(pieces, axis=1)

    def sample_window(inputs):
        charge, charge_step, cell_index, weights, slopes, values = inputs
        return sample_block(
            charge, charge_step, cell_index, weights, slopes, values, first_plane, plane_count
        )

    window_forces, derivative_part = lax.map(
        sample_window,
        (charges, charge_steps, index_windows, weight_windows, slope_windows, potential_field),
    )
    forces = jnp.moveaxis(window_forces, 0, 1)
    energy_total = lax.psum(energy_part, "slab")
    derivative_total = lax.psum(derivative_part, "slab")
    atom_total = atoms_here * slab_count
    return (forces, energy_total / atom_total, derivative_total / atom_total)


def solution(mesh):
    return jax.shard_map(
        body,
        mesh=mesh,
        in_specs=(
            P("win"),
            P("win", "slab"),
            P("win", "slab"),
            P("win", "slab"),
            P(None, "win", "slab"),
            P(None, None, "win", "slab"),
            P(None, None, "win", "slab"),
        ),
        out_specs=(P(None, "win", "slab"), P("win"), P("win")),
        check_vma=False,
    )
```

profile of v0, /device:TPU:0, one launch (start us, length us, event | category | flops | bytes accessed | tf_op | source)
XLA Modules:
  0.0 637.9 jit_solution(1168671799262427273)
XLA Ops:
  3.1 25.3 %while.26 = (s32[]{:T(128)}, f32[4,19,128,128]{2,3,1,0:T(8,128)}, s32[4,3,512]{2,1,0:T(4,128)S(1)}, s32[]{:T(128)}, f32[4,3,4,512]{3,2,1,0:T(4,128)S(1)}, /*inde...) while((s32[]{:T(128)}, f32[4,19,128,128]{2,3,1,0:T(8,128)}, ...), condition=%wide.region_1.2_spmd, body=%wide.region_0.1_spmd.sunk | while | flops 1915456512 | bytes 2517685 | solution.py:170
  30.7 12.5 %collective-permute-done = f32[4,3,128,128]{2,3,1,0:T(8,128)S(1)} collective-permute-done((f32[4,3,128,128]{2,3,1,0:T(8,128)S(1)}, f32[4,3,128,128]{2,3,1,0:T(8,128)S(1)}, u32[]{:S(2)}, u32[]{:S(2)}) %collective-permute-start) | collective-permute-done | bytes 786464 | tf_op jit(solution)/shard_map/ppermute | solution.py:20
  56.2 7.4 %fusion.108 = f32[4,16,128,128]{3,2,1,0:T(8,128)S(1)} fusion(f32[4,16,128,128]{3,2,1,0:T(8,128)S(1)} %fusion.130), kind=kOutput, calls=%fused_computation.248 | convolution fusion | flops 1611890688 | bytes 8388608 | tf_op jit(solution)/shard_map/wpkb,bl->wpkl/dot_general | solution.py:91
  67.6 7.5 %add_bitcast_fusion.3 = f32[4,1,16,128,128]{4,3,2,0,1:T(8,128)S(1)} fusion(f32[4,16,128,128]{3,2,1,0:T(8,128)S(1)} %fusion.110, f32[4,16,128,128]{3,2,1,0:T(8,128)S(1)} %fusion.131), kind=kOutput, calls=%fused_computation.264 | convolution fusion | flops 1611890688 | bytes 12582912 | tf_op jit(solution)/shard_map/wpkb,bl->wpkl/dot_general | solution.py:88
  83.3 8.1 %copy.64 = f32[4,2,16,128,128]{4,2,0,1,3:T(8,128)} copy(f32[4,2,16,128,128]{4,3,2,0,1:T(8,128)S(1)} %pad_maximum_fusion) | data formatting | bytes 16777216 | tf_op jit(solution)/shard_map/stack | solution.py:94
  97.1 93.5 %all-to-all-done = f32[4,2,16,128,128]{4,2,0,1,3:T(8,128)} async-done(((f32[4,2,16,128,128]{4,2,0,1,3:T(8,128)}), f32[4,2,16,128,128]{4,2,0,1,3:T(8,128)}, u32[]{:S(2)}, u32[]{:S(2)}) %all-to-all-start) | async-done | bytes 8388640 | tf_op jit(solution)/shard_map/all_to_all | solution.py:182
  190.6 8.2 %copy.66 = f32[4,2,8,16,16,128]{5,4,3,2,1,0:T(8,128)S(1)} copy(f32[4,2,8,16,16,128]{5,3,0,1,4,2:T(8,128)} %bitcast.86) | data formatting | bytes 16777216 | tf_op jit(solution)/shard_map/all_to_all | solution.py:182
  257.7 10.3 %copy.69 = f32[4,2,128,16,128]{4,3,0,1,2:T(8,128)} copy(f32[4,2,128,16,128]{2,4,3,0,1:T(8,128)} %pad_maximum_fusion.1) | data formatting | bytes 16777216 | tf_op jit(solution)/shard_map/stack | solution.py:146
  267.9 97.8 %all_to_all.36 = f32[4,2,128,16,128]{4,3,0,1,2:T(8,128)S(1)} all-to-all(f32[4,2,128,16,128]{4,3,0,1,2:T(8,128)} %copy.69), channel_id=1, replica_groups=mesh['win'=4,'slab'=8] {'slab'}, dimensions={2} | all-to-all | bytes 16777216 | tf_op jit(solution)/shard_map/all_to_all | solution.py:187
  399.1 9.4 %collective-permute-done.1 = f32[4,3,128,128]{2,3,1,0:T(8,128)S(1)} collective-permute-done((f32[4,3,128,128]{2,3,1,0:T(8,128)S(1)}, f32[4,3,128,128]{2,3,1,0:T(8,128)S(1)}, u32[]{:S(2)}, u32[]{:S(2)}) %collective-permute-start.1) | collective-permute-done | bytes 786464 | tf_op jit(solution)/shard_map/ppermute | solution.py:20
  413.5 209.0 %while.27 = (s32[]{:T(128)}, f32[4,3,512]{2,0,1:T(4,128)S(1)}, f32[4]{0:T(128)S(1)}, f32[4,512]{1,0:T(4,128)}, s32[4,3,512]{2,1,0:T(4,128)S(1)}, /*index=5*/s32[...) while((s32[]{:T(128)}, f32[4,3,512]{2,0,1:T(4,128)S(1)}, ...), condition=%wide.region_4.5_spmd, body=%wide.region_2.4_spmd.sunk | while | flops 3872960512 | bytes 29543656 | solution.py:202
  420.7 11.9 %fusion.328 = f32[512,1,19]{2,1,0:T(1,128)S(1)} fusion(f32[512,128,1]{1,2,0:T(1,128)S(1)} %bitcast.372, f32[512,19,128]{2,0,1:T(8,128)S(1)} %fusion.327), kind=kOutput, calls=%fused_computation.94.clone.1 | convolution fusion | flops 14942208 | bytes 5281792 | tf_op jit(solution)/shard_map/while/body/eval_jaxpr/ia,ipa->ip/dot_general | solution.py:76
  438.5 12.1 %fusion.329 = f32[512,1,19]{2,1,0:T(1,128)S(1)} fusion(f32[512,128,1]{1,2,0:T(1,128)S(1)} %bitcast.379, f32[512,19,128]{2,0,1:T(8,128)S(1)} %fusion.325), kind=kOutput, calls=%fused_computation.92.clone.1 | convolution fusion | flops 14942208 | bytes 5281792 | tf_op jit(solution)/shard_map/while/body/eval_jaxpr/ia,ipa->ip/dot_general | solution.py:74
  450.6 11.9 %fusion.326 = f32[512,1,19]{2,1,0:T(1,128)S(1)} fusion(f32[512,128,1]{1,2,0:T(1,128)S(1)} %bitcast.373, f32[512,19,128]{2,0,1:T(8,128)S(1)} %fusion.325), kind=kOutput, calls=%fused_computation.90.clone.1 | convolution fusion | flops 14942208 | bytes 5281792 | tf_op jit(solution)/shard_map/while/body/eval_jaxpr/ia,ipa->ip/dot_general | solution.py:73
  472.6 12.1 %fusion.328 = f32[512,1,19]{2,1,0:T(1,128)S(1)} fusion(f32[512,128,1]{1,2,0:T(1,128)S(1)} %bitcast.372, f32[512,19,128]{2,0,1:T(8,128)S(1)} %fusion.327), kind=kOutput, calls=%fused_computation.94.clone.1 | convolution fusion | flops 14942208 | bytes 5281792 | tf_op jit(solution)/shard_map/while/body/eval_jaxpr/ia,ipa->ip/dot_general | solution.py:76
  490.7 11.9 %fusion.329 = f32[512,1,19]{2,1,0:T(1,128)S(1)} fusion(f32[512,128,1]{1,2,0:T(1,128)S(1)} %bitcast.379, f32[512,19,128]{2,0,1:T(8,128)S(1)} %fusion.325), kind=kOutput, calls=%fused_computation.92.clone.1 | convolution fusion | flops 14942208 | bytes 5281792 | tf_op jit(solution)/shard_map/while/body/eval_jaxpr/ia,ipa->ip/dot_general | solution.py:74
  502.5 11.9 %fusion.326 = f32[512,1,19]{2,1,0:T(1,128)S(1)} fusion(f32[512,128,1]{1,2,0:T(1,128)S(1)} %bitcast.373, f32[512,19,128]{2,0,1:T(8,128)S(1)} %fusion.325), kind=kOutput, calls=%fused_computation.90.clone.1 | convolution fusion | flops 14942208 | bytes 5281792 | tf_op jit(solution)/shard_map/while/body/eval_jaxpr/ia,ipa->ip/dot_general | solution.py:73
  524.7 11.9 %fusion.328 = f32[512,1,19]{2,1,0:T(1,128)S(1)} fusion(f32[512,128,1]{1,2,0:T(1,128)S(1)} %bitcast.372, f32[512,19,128]{2,0,1:T(8,128)S(1)} %fusion.327), kind=kOutput, calls=%fused_computation.94.clone.1 | convolution fusion | flops 14942208 | bytes 5281792 | tf_op jit(solution)/shard_map/while/body/eval_jaxpr/ia,ipa->ip/dot_general | solution.py:76
  542.6 11.9 %fusion.329 = f32[512,1,19]{2,1,0:T(1,128)S(1)} fusion(f32[512,128,1]{1,2,0:T(1,128)S(1)} %bitcast.379, f32[512,19,128]{2,0,1:T(8,128)S(1)} %fusion.325), kind=kOutput, calls=%fused_computation.92.clone.1 | convolution fusion | flops 14942208 | bytes 5281792 | tf_op jit(solution)/shard_map/while/body/eval_jaxpr/ia,ipa->ip/dot_general | solution.py:74
  554.5 12.1 %fusion.326 = f32[512,1,19]{2,1,0:T(1,128)S(1)} fusion(f32[512,128,1]{1,2,0:T(1,128)S(1)} %bitcast.373, f32[512,19,128]{2,0,1:T(8,128)S(1)} %fusion.325), kind=kOutput, calls=%fused_computation.90.clone.1 | convolution fusion | flops 14942208 | bytes 5281792 | tf_op jit(solution)/shard_map/while/body/eval_jaxpr/ia,ipa->ip/dot_general | solution.py:73
  576.6 11.9 %fusion.328 = f32[512,1,19]{2,1,0:T(1,128)S(1)} fusion(f32[512,128,1]{1,2,0:T(1,128)S(1)} %bitcast.372, f32[512,19,128]{2,0,1:T(8,128)S(1)} %fusion.327), kind=kOutput, calls=%fused_computation.94.clone.1 | convolution fusion | flops 14942208 | bytes 5281792 | tf_op jit(solution)/shard_map/while/body/eval_jaxpr/ia,ipa->ip/dot_general | solution.py:76
  594.5 12.1 %fusion.329 = f32[512,1,19]{2,1,0:T(1,128)S(1)} fusion(f32[512,128,1]{1,2,0:T(1,128)S(1)} %bitcast.379, f32[512,19,128]{2,0,1:T(8,128)S(1)} %fusion.325), kind=kOutput, calls=%fused_computation.92.clone.1 | convolution fusion | flops 14942208 | bytes 5281792 | tf_op jit(solution)/shard_map/while/body/eval_jaxpr/ia,ipa->ip/dot_general | solution.py:74
  606.6 11.9 %fusion.326 = f32[512,1,19]{2,1,0:T(1,128)S(1)} fusion(f32[512,128,1]{1,2,0:T(1,128)S(1)} %bitcast.373, f32[512,19,128]{2,0,1:T(8,128)S(1)} %fusion.325), kind=kOutput, calls=%fused_computation.90.clone.1 | convolution fusion | flops 14942208 | bytes 5281792 | tf_op jit(solution)/shard_map/while/body/eval_jaxpr/ia,ipa->ip/dot_general | solution.py:73
  622.5 14.6 %all-reduce.1 = (f32[4]{0:T(128)S(1)}, f32[4]{0:T(128)S(1)}) all-reduce(f32[4]{0:T(128)S(1)} %broadcast_multiply_fusion.2, f32[4]{0:T(128)S(1)} %get-tuple-element.210), channel_id=1, replica_groups=mesh['win'=4,'slab'=8] {'slab'}, use_global_device_ids=true, to_apply=%region_6.7 | all-reduce | flops 8 | bytes 64 | tf_op jit(solution)/shard_map/psum | solution.py:207
  (170 shorter events, 221.0 us)
Async XLA Ops:
  28.4 20.9 %copy-start.4 = (f32[4,512]{1,0:T(4,128)}, f32[4,512]{1,0:T(4,128)S(1)}, u32[]{:S(2)}) copy-start(f32[4,512]{1,0:T(4,128)S(1)} %get-tuple-element.728) | copy-start | bytes 24580
  29.6 13.6 %collective-permute-start = (f32[4,3,128,128]{2,3,1,0:T(8,128)S(1)}, f32[4,3,128,128]{2,3,1,0:T(8,128)S(1)}, u32[]{:S(2)}, u32[]{:S(2)}) collective-permute-start(f32[4,3,128,128]{2,3,1,0:T(8,128)S(1)} %slice.373), channel_id=1, source_target_pairs={{0,1},{1,2},{2,3},{3,4},{4,5},{5,6},{6,7},{7,0},{8,9},{9,10},{10,1... | collective-permute-start | bytes 2359304 | tf_op jit(solution)/shard_map/ppermute | solution.py:20
  49.3 14.4 %slice-start = ((s8[4980736]{0:T(1024)(128)(4,1)}), s8[4194304]{0:T(1024)(128)(4,1)S(1)}, s32[]{:S(2)}) async-start(s8[4980736]{0:T(1024)(128)(4,1)} %bitcast.380), calls=%async_computation.2 | async-start | bytes 8388608
  56.2 7.5 %slice-start.1 = ((s8[4980736]{0:T(1024)(128)(4,1)}), s8[786432]{0:T(1024)(128)(4,1)S(1)}, s32[]{:S(2)}) async-start(s8[4980736]{0:T(1024)(128)(4,1)} %bitcast.380), calls=%async_computation.3 | async-start | bytes 1572864
  91.4 99.2 %all-to-all-start = ((f32[4,2,16,128,128]{4,2,0,1,3:T(8,128)}), f32[4,2,16,128,128]{4,2,0,1,3:T(8,128)}, u32[]{:S(2)}, u32[]{:S(2)}) async-start(f32[4,2,16,128,128]{4,2,0,1,3:T(8,128)} %copy.64), calls=%async_computation | async-start | bytes 16777216 | tf_op jit(solution)/shard_map/all_to_all | solution.py:182
  208.0 7.3 %copy-start.1 = (f32[4,1,128,16,128]{2,4,3,0,1:T(8,128)S(1)}, f32[4,1,128,16,128]{2,4,3,0,1:T(8,128)}, u32[]{:S(2)}) copy-start(f32[4,1,128,16,128]{2,4,3,0,1:T(8,128)} %copy.119) | copy-start | bytes 12582916
  236.8 4.0 copy-start
  236.8 4.0 copy-start.3
  389.9 9.2 %copy-start.5 = (f32[3,4,4,512]{3,2,1,0:T(4,128)S(1)}, f32[3,4,4,512]{3,2,1,0:T(4,128)}, u32[]{:S(2)}) copy-start(f32[3,4,4,512]{3,2,1,0:T(4,128)} %param.17) | copy-start | bytes 294916
  396.9 2.0 copy-start.2
  399.0 9.6 %collective-permute-start.1 = (f32[4,3,128,128]{2,3,1,0:T(8,128)S(1)}, f32[4,3,128,128]{2,3,1,0:T(8,128)S(1)}, u32[]{:S(2)}, u32[]{:S(2)}) collective-permute-start(f32[4,3,128,128]{2,3,1,0:T(8,128)S(1)} %slice.383), channel_id=1, source_target_pairs={{0,7},{1,0},{2,1},{3,2},{4,3},{5,4},{6,5},{7,6},{8,15},{9,8},{10,9... | collective-permute-start | bytes 2359304 | tf_op jit(solution)/shard_map/ppermute | solution.py:20
  622.5 15.1 %copy-start.6 = (f32[4,3,512]{2,0,1:T(4,128)}, f32[4,3,512]{2,0,1:T(4,128)S(1)}, u32[]{:S(2)}) copy-start(f32[4,3,512]{2,0,1:T(4,128)S(1)} %get-tuple-element.209) | copy-start | bytes 73732
where the time goes:
time: 643 us; the launch traced here: 638 us
  matrix products  322 us (50%)
  waiting for transfers between devices  115 us (18%)
  blocking collectives  112 us (17%)
  local copies, waits for them, and re-layouts  52.8 us (8%)
  other arithmetic  25.1 us (4%)
    all_to_all x1, blocking collectives, body(): lax.all_to_all(stacked, 'slab', split_axis=2, concat_axis=3, tiled=True)  97.8 us
    all_to_all x1, waiting for transfers between devices, body(): lax.all_to_all(slab_spectrum, 'slab', split_axis=3, concat_axis=2, tiled=...  93.5 us
    dot_general x4, matrix products, sample_block(): jnp.einsum('ia,ipa->ip', steep_x, along_rows, precision=highest)  48 us
    dot_general x4, matrix products, sample_block(): jnp.einsum('ia,ipa->ip', rows_x, along_steep, precision=highest)  47.8 us
    dot_general x4, matrix products, sample_block(): reduced = jnp.einsum('ia,ipa->ip', rows_x, along_rows, precision=highest)  47.8 us
    dot_general x4, matrix products, sample_block(): along_steep = jnp.einsum('pab,ib->ipa', values, steep_y, precision=highest)  23.8 us
    dot_general x4, matrix products, sample_block(): along_rows = jnp.einsum('pab,ib->ipa', values, rows_y, precision=highest)  23.8 us
    ppermute x2, waiting for transfers between devices, passed_along(): return lax.ppermute(value, axis, pairs)  22 us
  transfers between devices with their start and end apart: 3, of which 3 were waited for; matrix products, arithmetic and copies ran while one was open for 0% of the time, Pallas kernels for 0%

commit v1 on v0

v1 whole, which is shorter than its diff:
```python
import functools

import jax
import jax.numpy as jnp
import numpy as np
from jax import lax
from jax.experimental import pallas as pl
from jax.experimental.pallas import tpu as pltpu
from jax.sharding import PartitionSpec as P

NX = 128
NY = 128
NZ = 128
REACH = 3

gauss_width = 2.0

CHARGE, STEP, CELL_X, CELL_Y, CELL_Z = 0, 1, 2, 3, 4
WX, WY, WZ, SX, SY, SZ = 8, 12, 16, 20, 24, 28
ROWS = 32


def passed_along(value, axis, steps):
    count = lax.axis_size(axis)
    pairs = [(source, (source + steps) % count) for source in range(count)]
    return lax.ppermute(value, axis, pairs)


def trig(length):
    counter = np.arange(length)
    angles = (np.outer(counter, counter) % length) * (2.0 * np.pi / length)
    return np.cos(angles), np.sin(angles)


def halves(table):
    table = table.astype(np.float32)
    high = table.astype(jnp.bfloat16)
    low = (table - high.astype(np.float32)).astype(jnp.bfloat16)
    return jnp.asarray(np.stack([high, low]))


def split(value):
    high = value.astype(jnp.bfloat16)
    return high, (value - high.astype(jnp.float32)).astype(jnp.bfloat16)


def dot3(left, right, dims=((1,), (0,))):
    one = functools.partial(
        lax.dot_general, dimension_numbers=(dims, ((), ())), preferred_element_type=jnp.float32
    )
    return one(left[0], right[0]) + (one(left[0], right[1]) + one(left[1], right[0]))


def stencil_rows(record, cell_row, weight_row, length):
    first = record[cell_row : cell_row + 1].astype(jnp.int32)
    cells = lax.broadcasted_iota(jnp.int32, (length, record.shape[1]), 0)
    away = cells - first
    away = jnp.where(away < 0, away + length, away)
    result = jnp.zeros(away.shape, jnp.float32)
    for offset in range(4):
        row = weight_row + offset
        result = jnp.where(away == offset, record[row : row + 1], result)
    return result


def plane_row(record, weight_row, plane, shift):
    away = plane + shift - record[CELL_Z : CELL_Z + 1].astype(jnp.int32)
    result = jnp.zeros(away.shape, jnp.float32)
    for offset in range(4):
        row = weight_row + offset
        result = jnp.where(away == offset, record[row : row + 1], result)
    return result


def planes_reached(distance, depth):
    if distance == 0:
        return depth
    return min(depth, depth + REACH - distance * depth)


def spread_kernel(depth, columns, native, atoms_ref, ty_ref, tx_ref, out_ref, grid_ref):
    sets = atoms_ref.shape[0]
    for part in range(2):
        lanes = slice(part * NY, (part + 1) * NY)
        for distance in range(sets):
            record = atoms_ref[distance, part]
            rows_x = stencil_rows(record, CELL_X, WX, NX)
            rows_y = split(stencil_rows(record, CELL_Y, WY, NY))
            charge = record[CHARGE : CHARGE + 1]

            def one_plane(plane, carry):
                strength = plane_row(record, WZ, plane, distance * depth) * charge
                spread = dot3(split(rows_x * strength), rows_y, ((1,), (1,)))
                if distance == 0:
                    grid_ref[plane, :, lanes] = spread
                else:
                    grid_ref[plane, :, lanes] += spread
                return carry

            lax.fori_loop(0, planes_reached(distance, depth), one_plane, 0)

    table_y = (ty_ref[0], ty_ref[1])
    table_x = (tx_ref[0], tx_ref[1])

    def transform(plane, carry):
        along_y = dot3(split(grid_ref[plane]), table_y)
        real, imaginary = along_y[:, :NY], along_y[:, NY:]
        stacked = jnp.concatenate(
            [along_y, jnp.concatenate([imaginary, -real], axis=1)], axis=0
        )
        both = dot3(table_x, split(stacked))
        for part in range(2):
            lanes = slice(part * NY, (part + 1) * NY)
            if native:
                for owner in range(NX // columns):
                    out_ref[owner, part, pl.ds(plane, columns, stride=depth), :] = both[
                        owner * columns : (owner + 1) * columns, lanes
                    ]
            else:
                out_ref[plane, part] = both[:, lanes]
        return carry

    lax.fori_loop(0, depth, transform, 0)


def column_kernel(columns, in_ref, influence_ref, forward_ref, inverse_ref, out_ref):
    sources = in_ref.shape[0]
    depth = in_ref.shape[2] // columns
    group = 2 if columns % 2 == 0 else 1
    forward = (forward_ref[0], forward_ref[1])
    inverse = (inverse_ref[0], inverse_ref[1])

    def one_group(step, carry):
        sides = []
        for k in range(group):
            start = pl.multiple_of((step * group + k) * depth, depth)
            sides.append(
                jnp.concatenate(
                    [
                        in_ref[source, part, pl.ds(start, depth), :]
                        for part in range(2)
                        for source in range(sources)
                    ],
                    axis=0,
                )
            )
        spectrum = dot3(forward, split(jnp.concatenate(sides, axis=1)))
        factor = jnp.concatenate([influence_ref[step * group + k] for k in range(group)], axis=1)
        scaled = spectrum * jnp.concatenate([factor, factor], axis=0)
        back = dot3(inverse, split(scaled))
        for k in range(group):
            start = pl.multiple_of((step * group + k) * depth, depth)
            for part in range(2):
                for source in range(sources):
                    top = part * NZ + source * depth
                    out_ref[source, part, pl.ds(start, depth), :] = back[
                        top : top + depth, k * NY : (k + 1) * NY
                    ]
        return carry

    lax.fori_loop(0, columns // group, one_group, 0)


def sample_kernel(
    depth, columns, native, in_ref, atoms_ref, ty_ref, tx_ref, out_ref, high_ref, low_ref, sums_ref
):
    sets = atoms_ref.shape[0]
    atoms = atoms_ref.shape[3]
    table_y = (ty_ref[0], ty_ref[1])
    table_x = (tx_ref[0], tx_ref[1])

    def transform(plane, carry):
        pieces = []
        for part in range(2):
            if native:
                pieces.append(
                    jnp.concatenate(
                        [
                            in_ref[owner, part, pl.ds(plane, columns, stride=depth), :]
                            for owner in range(NX // columns)
                        ],
                        axis=0,
                    )
                )
            else:
                pieces.append(in_ref[plane, part])
        real, imaginary = pieces
        stacked = jnp.concatenate(
            [
                jnp.concatenate([real, imaginary], axis=1),
                jnp.concatenate([-imaginary, real], axis=1),
            ],
            axis=0,
        )
        along_x = dot3(table_x, split(stacked))
        high, low = split(dot3(split(along_x), table_y))
        high_ref[plane] = high
        low_ref[plane] = low
        return carry

    lax.fori_loop(0, depth, transform, 0)

    for part in range(2):
        lanes = slice(part * NY, (part + 1) * NY)
        for distance in range(sets):
            record = atoms_ref[distance, part]
            rows_y = split(stencil_rows(record, CELL_Y, WY, NY))
            steep_y = split(stencil_rows(record, CELL_Y, SY, NY))
            sums_ref[...] = jnp.zeros(sums_ref.shape, jnp.float32)

            def one_plane(plane, carry):
                values = (high_ref[plane, :, lanes], low_ref[plane, :, lanes])
                weight = plane_row(record, WZ, plane, distance * depth)
                slope = plane_row(record, SZ, plane, distance * depth)
                along = dot3(values, rows_y)
                sums_ref[0] += weight * along
                sums_ref[1] += slope * along
                sums_ref[2] += weight * dot3(values, steep_y)
                return carry

            lax.fori_loop(0, planes_reached(distance, depth), one_plane, 0)
            rows_x = stencil_rows(record, CELL_X, WX, NX)
            steep_x = stencil_rows(record, CELL_X, SX, NX)
            charge = record[CHARGE : CHARGE + 1]
            level = sums_ref[0]

            def total(value):
                return jnp.sum(value, axis=0, keepdims=True)

            out_ref[distance, part] = jnp.concatenate(
                [
                    total(rows_x * level),
                    -charge * total(steep_x * level),
                    -charge * total(rows_x * sums_ref[2]),
                    -charge * total(rows_x * sums_ref[1]),
                    jnp.zeros((4, atoms), jnp.float32),
                ],
                axis=0,
            )


def influence_block(first_column, column_count):
    def frequency(counter, length):
        return jnp.where(counter >= length // 2, counter - length, counter).astype(
            jnp.float32
        ) / length

    freq_x = frequency(first_column + jnp.arange(column_count, dtype=jnp.int32), NX)[:, None, None]
    freq_z = frequency(jnp.arange(NZ, dtype=jnp.int32), NZ)[None, :, None]
    freq_y = frequency(jnp.arange(NY, dtype=jnp.int32), NY)[None, None, :]
    squared = freq_z * freq_z + freq_x * freq_x + freq_y * freq_y
    positive = squared > 0
    safe_value = jnp.where(positive, squared, jnp.float32(1.0))
    return jnp.where(
        positive,
        jnp.exp(-gauss_width * squared) / (np.pi * NX * NY * NZ * safe_value),
        jnp.float32(0.0),
    )


def body(lambdas, charge_a, charge_b, perturbed, grid_index, spline_weights, spline_slopes):
    windows, atoms = charge_a.shape
    slabs = lax.axis_size("slab")
    depth = NZ // slabs
    columns = NX // slabs
    native = depth % 8 == 0 and columns % 8 == 0
    me = lax.axis_index("slab")
    flags = perturbed.astype(jnp.float32)
    steps = flags * (charge_b - charge_a)
    charges = charge_a + flags * lambdas[:, None] * (charge_b - charge_a)

    cells = jnp.stack([grid_index[0], grid_index[1], grid_index[2] - me * depth], axis=1)
    blank = jnp.zeros((windows, 3, atoms), jnp.float32)
    record = jnp.concatenate(
        [charges[:, None], steps[:, None], cells.astype(jnp.float32), blank]
        + [jnp.moveaxis(spline_weights[d], 1, 0) for d in range(3)]
        + [jnp.moveaxis(spline_slopes[d], 1, 0) for d in range(3)],
        axis=1,
    )
    if windows % 2:
        record = jnp.pad(record, ((0, 1), (0, 0), (0, 0)))
    groups = record.shape[0] // 2
    reach = -(-REACH // depth)
    records = jnp.stack(
        [record] + [passed_along(record, "slab", distance) for distance in range(1, reach + 1)]
    )

    cos_x, sin_x = trig(NX)
    cos_y, sin_y = trig(NY)
    cos_z, sin_z = trig(NZ)
    table_x = halves(np.block([cos_x, sin_x]))
    forward_y = halves(np.block([[cos_y, -sin_y], [sin_y, cos_y]]))
    inverse_y = halves(np.block([[cos_y, sin_y], [-sin_y, cos_y]]))
    forward_z = halves(np.block([[cos_z, sin_z], [-sin_z, cos_z]]))
    inverse_z = halves(np.block([[cos_z, -sin_z], [sin_z, cos_z]]))
    influence = influence_block(me * columns, columns)

    if native:
        slab_shape = (slabs, 2, columns * depth, NY)
    else:
        slab_shape = (depth, 2, NX, NY)
    column_shape = (slabs, 2, columns * depth, NY) if native else (1, 2, columns * NZ, NY)

    cost = pl.CostEstimate(flops=8 * 10**9, bytes_accessed=4 * 10**6, transcendentals=0)

    def call(kernel, shape, scratch=()):
        return pl.pallas_call(
            kernel,
            out_shape=jax.ShapeDtypeStruct(shape, jnp.float32),
            scratch_shapes=scratch,
            cost_estimate=cost,
        )

    def to_columns(value):
        if native:
            return lax.all_to_all(value, "slab", 0, 0, tiled=True)
        value = lax.all_to_all(value, "slab", 2, 0, tiled=True)
        return jnp.transpose(value, (1, 2, 0, 3)).reshape(column_shape)

    def to_planes(value):
        if native:
            return lax.all_to_all(value, "slab", 0, 0, tiled=True)
        value = jnp.transpose(value.reshape(2, columns, NZ, NY), (2, 0, 1, 3))
        return lax.all_to_all(value, "slab", 0, 2, tiled=True)

    sampled = []
    for group in range(groups):
        mine = records[:, 2 * group : 2 * group + 2]
        planes = call(
            functools.partial(spread_kernel, depth, columns, native),
            slab_shape,
            [pltpu.VMEM((depth, NX, 2 * NY), jnp.float32)],
        )(mine, forward_y, table_x)
        back = call(functools.partial(column_kernel, columns), column_shape)(
            to_columns(planes), influence, forward_z, inverse_z
        )
        sampled.append(
            call(
                functools.partial(sample_kernel, depth, columns, native),
                (reach + 1, 2, 8, atoms),
                [
                    pltpu.VMEM((depth, NX, 2 * NY), jnp.bfloat16),
                    pltpu.VMEM((depth, NX, 2 * NY), jnp.bfloat16),
                    pltpu.VMEM((3, NX, atoms), jnp.float32),
                ],
            )(to_planes(back), mine, inverse_y, table_x)
        )
    results = jnp.concatenate(sampled, axis=1)[:, :windows]
    partial_sums = jnp.sum(
        results[:, :, :1] * records[:, :windows, CHARGE : STEP + 1], axis=(0, 3)
    )
    sums = jnp.sum(lax.all_gather(partial_sums, "slab"), axis=0)
    forces = results[0, :, 1:4]
    for distance in range(1, reach + 1):
        forces = forces + passed_along(results[distance, :, 1:4], "slab", -distance)
    total = atoms * slabs
    return (jnp.moveaxis(forces, 1, 0), 0.5 * sums[:, 0] / total, sums[:, 1] / total)


def solution(mesh):
    return jax.shard_map(
        body,
        mesh=mesh,
        in_specs=(
            P("win"),
            P("win", "slab"),
            P("win", "slab"),
            P("win", "slab"),
            P(None, "win", "slab"),
            P(None, None, "win", "slab"),
            P(None, None, "win", "slab"),
        ),
        out_specs=(P(None, "win", "slab"), P("win"), P("win")),
        check_vma=False,
    )
```

time: 643 us -> 204 us (0.32)
  matrix products: 322 us -> 0 us
  Pallas kernels: 0 us -> 115 us
  blocking collectives: 112 us -> 9.16 us
  waiting for transfers between devices: 115 us -> 46.5 us
  local copies, waits for them, and re-layouts: 52.8 us -> 6.68 us
  other arithmetic: 25.1 us -> 7.01 us
  starting transfers between devices: 6.25 us -> 17.3 us
    dot_general x44 -> x0, matrix products: 322 us -> none  [the longest x4 48 us: sample_block(): jnp.einsum('ia,ipa->ip', steep_x, along_rows, precision=highest)]
    pallas_call x0 -> x6, Pallas kernels: none -> 115 us  [the longest x2 53.1 us: body(): call(functools.partial(sample_kernel, depth, columns, native), (reach + 1...]
    all_to_all x1 -> x0, blocking collectives: 97.8 us -> none  [body(): lax.all_to_all(stacked, 'slab', split_axis=2, concat_axis=3, tiled=True)]
    all_to_all x1 -> x4, waiting for transfers between devices: 93.5 us -> 38.5 us  [the longest x2 20.6 us: to_columns(): return lax.all_to_all(value, 'slab', 0, 0, tiled=True)]
    another operation x2 -> x0, local copies, waits for them, and re-layouts: 18.4 us -> none  [the longest x1 10.3 us: column_transform(): return (jnp.stack([back_real, back_imaginary], axis=1), energy_part)]
    psum x1 -> x0, blocking collectives: 14.6 us -> none  [body(): energy_total = lax.psum(energy_part, 'slab')]
    ppermute x2, waiting for transfers between devices: 22 us -> 8.01 us  [passed_along(): return lax.ppermute(value, axis, pairs)]
    all_to_all x1 -> x4, starting transfers between devices: 5.13 us -> 15.3 us  [the longest x2 8.14 us: to_planes(): return lax.all_to_all(value, 'slab', 0, 0, tiled=True)]
  transfers between devices with their start and end apart: 3 -> 6, of which waited for: 3 -> 5; matrix products, arithmetic and copies ran while one was open for 0% -> 1% of each run, Pallas kernels for 0% -> 33%
where the time goes in v1:
time: 204 us; the launch traced here: 202 us
  Pallas kernels  115 us (56%)
  waiting for transfers between devices  46.5 us (23%)
  starting transfers between devices  17.3 us (8%)
  blocking collectives  9.16 us (4%)
  other arithmetic  7.01 us (3%)
  local copies, waits for them, and re-layouts  6.68 us (3%)
    pallas_call x2, Pallas kernels, body(): call(functools.partial(sample_kernel, depth, columns, native), (reach + 1...  53.1 us
    pallas_call x2, Pallas kernels, body(): call(functools.partial(spread_kernel, depth, columns, native), slab_shape...  44.4 us
    all_to_all x2, waiting for transfers between devices, to_columns(): return lax.all_to_all(value, 'slab', 0, 0, tiled=True)  20.6 us
    all_to_all x2, waiting for transfers between devices, to_planes(): return lax.all_to_all(value, 'slab', 0, 0, tiled=True)  17.9 us
    pallas_call x2, Pallas kernels, body(): call(functools.partial(column_kernel, columns), column_shape)  17.5 us
    all_gather x1, blocking collectives, body(): sums = jnp.sum(lax.all_gather(partial_sums, 'slab'), axis=0)  9.16 us
    all_to_all x2, starting transfers between devices, to_planes(): return lax.all_to_all(value, 'slab', 0, 0, tiled=True)  8.14 us
    ppermute x2, waiting for transfers between devices, passed_along(): return lax.ppermute(value, axis, pairs)  8.01 us
  transfers between devices with their start and end apart: 6, of which 5 were waited for; matrix products, arithmetic and copies ran while one was open for 1% of the time, Pallas kernels for 33%

profile of v1, /device:TPU:0, one launch (start us, length us, event | category | flops | bytes accessed | tf_op | source)
XLA Modules:
  0.0 202.5 jit_solution(17900686847137771818)
XLA Ops:
  0.6 0.8 convert_multiply_fusion
  4.7 6.9 %collective-permute-done = f32[4,32,512]{2,1,0:T(8,128)S(1)} collective-permute-done((f32[4,32,512]{2,1,0:T(8,128)S(1)}, f32[4,32,512]{2,1,0:T(8,128)S(1)}, u32[]{:S(2)}, u32[]{:S(2)}) %collective-permute-start) | collective-permute-done | bytes 262176 | tf_op jit(solution)/shard_map/ppermute | solution.py:26
  11.6 0.8 fusion.5
  12.5 22.2 %shard_map.139 = f32[8,2,256,128]{3,2,1,0:T(8,128)} custom-call(f32[2,2,32,512]{3,2,1,0:T(8,128)} %get-tuple-element.9.atoms_ref, bf16[2,256,256]{2,1,0:T(8,128)(2,1)} %constant.43.clone.ty_ref.inverse_ref, bf16[2,128,256]{2,1,0:T(8,128)(2,1)} %constant.42.clone.tx_ref), custom_call_target="tpu_custom_call" | custom-call | flops 8000000000 | bytes 4000000 | tf_op jit(solution)/shard_map/pallas_call | solution.py:329
  34.7 3.6 %all-to-all-start = ((f32[8,2,256,128]{3,2,1,0:T(8,128)}), f32[8,2,256,128]{3,2,1,0:T(8,128)S(1)}, u32[]{:S(2)}, u32[]{:S(2)}) async-start(f32[8,2,256,128]{3,2,1,0:T(8,128)} %shard_map.139), calls=%async_computation | async-start | bytes 4194304 | tf_op jit(solution)/shard_map/all_to_all | solution.py:316
  38.3 22.2 %shard_map.142 = f32[8,2,256,128]{3,2,1,0:T(8,128)} custom-call(f32[2,2,32,512]{3,2,1,0:T(8,128)} %get-tuple-element.10.atoms_ref, bf16[2,256,256]{2,1,0:T(8,128)(2,1)} %constant.43.clone.ty_ref.inverse_ref, bf16[2,128,256]{2,1,0:T(8,128)(2,1)} %constant.42.clone.tx_ref), custom_call_target="tpu_custom_call" | custom-call | flops 8000000000 | bytes 4000000 | tf_op jit(solution)/shard_map/pallas_call | solution.py:329
  60.5 4.4 %all-to-all-done.in_ref = f32[8,2,256,128]{3,2,1,0:T(8,128)S(1)} async-done(((f32[8,2,256,128]{3,2,1,0:T(8,128)}), f32[8,2,256,128]{3,2,1,0:T(8,128)S(1)}, u32[]{:S(2)}, u32[]{:S(2)}) %all-to-all-start) | async-done | bytes 2097184 | tf_op jit(solution)/shard_map/all_to_all | solution.py:316
  64.9 1.4 copy-done.1
  66.2 3.6 %all-to-all-start.2 = ((f32[8,2,256,128]{3,2,1,0:T(8,128)}), f32[8,2,256,128]{3,2,1,0:T(8,128)S(1)}, u32[]{:S(2)}, u32[]{:S(2)}) async-start(f32[8,2,256,128]{3,2,1,0:T(8,128)} %shard_map.142), calls=%async_computation.2 | async-start | bytes 4194304 | tf_op jit(solution)/shard_map/all_to_all | solution.py:316
  70.0 1.5 fusion.influence_ref
  71.4 8.7 %shard_map.140 = f32[8,2,256,128]{3,2,1,0:T(8,128)} custom-call(f32[8,2,256,128]{3,2,1,0:T(8,128)} %copy-done.1, f32[16,128,128]{2,1,0:T(8,128)} %fusion.influence_ref, bf16[2,256,256]{2,1,0:T(8,128)(2,1)} %constant.44.clone.forward_ref.ty_ref, bf16[2,256,256]{2,1,0:T(8,128)(2,1)} %constant.43.clone.ty_ref.inverse_ref), custom_call_target="tpu_custom_call" | custom-call | flops 8000000000 | bytes 4000000 | tf_op jit(solution)/shard_map/pallas_call | solution.py:334
  80.2 16.2 %all-to-all-done.2.in_ref = f32[8,2,256,128]{3,2,1,0:T(8,128)S(1)} async-done(((f32[8,2,256,128]{3,2,1,0:T(8,128)}), f32[8,2,256,128]{3,2,1,0:T(8,128)S(1)}, u32[]{:S(2)}, u32[]{:S(2)}) %all-to-all-start.2) | async-done | bytes 2097184 | tf_op jit(solution)/shard_map/all_to_all | solution.py:316
  96.4 1.4 copy-done
  97.8 4.4 %all-to-all-start.1 = ((f32[8,2,256,128]{3,2,1,0:T(8,128)}), f32[8,2,256,128]{3,2,1,0:T(8,128)}, u32[]{:S(2)}, u32[]{:S(2)}) async-start(f32[8,2,256,128]{3,2,1,0:T(8,128)} %shard_map.140), calls=%async_computation.1 | async-start | bytes 4194304 | tf_op jit(solution)/shard_map/all_to_all | solution.py:322
  102.1 8.8 %shard_map.143 = f32[8,2,256,128]{3,2,1,0:T(8,128)} custom-call(f32[8,2,256,128]{3,2,1,0:T(8,128)} %copy-done, f32[16,128,128]{2,1,0:T(8,128)} %fusion.influence_ref, bf16[2,256,256]{2,1,0:T(8,128)(2,1)} %constant.44.clone.forward_ref.ty_ref, bf16[2,256,256]{2,1,0:T(8,128)(2,1)} %constant.43.clone.ty_ref.inverse_ref), custom_call_target="tpu_custom_call" | custom-call | flops 8000000000 | bytes 4000000 | tf_op jit(solution)/shard_map/pallas_call | solution.py:334
  110.9 17.9 %all-to-all-done.1.in_ref = f32[8,2,256,128]{3,2,1,0:T(8,128)} async-done(((f32[8,2,256,128]{3,2,1,0:T(8,128)}), f32[8,2,256,128]{3,2,1,0:T(8,128)}, u32[]{:S(2)}, u32[]{:S(2)}) %all-to-all-start.1) | async-done | bytes 2097184 | tf_op jit(solution)/shard_map/all_to_all | solution.py:322
  128.8 3.8 %all-to-all-start.3 = ((f32[8,2,256,128]{3,2,1,0:T(8,128)}), f32[8,2,256,128]{3,2,1,0:T(8,128)S(1)}, u32[]{:S(2)}, u32[]{:S(2)}) async-start(f32[8,2,256,128]{3,2,1,0:T(8,128)} %shard_map.143), calls=%async_computation.3 | async-start | bytes 4194304 | tf_op jit(solution)/shard_map/all_to_all | solution.py:322
  132.5 26.6 %shard_map.141 = f32[2,2,8,512]{3,2,1,0:T(8,128)} custom-call(f32[8,2,256,128]{3,2,1,0:T(8,128)} %all-to-all-done.1.in_ref, f32[2,2,32,512]{3,2,1,0:T(8,128)} %get-tuple-element.9.atoms_ref, bf16[2,256,256]{2,1,0:T(8,128)(2,1)} %constant.44.clone.forward_ref.ty_ref, bf16[2,128,256]{2,1,0:T(8,128)(2,1)} %constant.42.clone.tx_ref), custom_call_target="tpu_custom_call" | custom-call | flops 8000000000 | bytes 4000000 | tf_op jit(solution)/shard_map/pallas_call | solution.py:338
  159.1 1.3 copy-done.2
  160.4 26.6 %shard_map.144 = f32[2,2,8,512]{3,2,1,0:T(8,128)} custom-call(f32[8,2,256,128]{3,2,1,0:T(8,128)} %copy-done.2, f32[2,2,32,512]{3,2,1,0:T(8,128)} %get-tuple-element.10.atoms_ref, bf16[2,256,256]{2,1,0:T(8,128)(2,1)} %constant.44.clone.forward_ref.ty_ref, bf16[2,128,256]{2,1,0:T(8,128)(2,1)} %constant.42.clone.tx_ref), custom_call_target="tpu_custom_call" | custom-call | flops 8000000000 | bytes 4000000 | tf_op jit(solution)/shard_map/pallas_call | solution.py:338
  187.0 0.8 pad_maximum_fusion.1
  188.8 9.2 %all-gather.1 = f32[8,4,2]{1,2,0:T(2,128)S(1)} all-gather(f32[1,4,2]{1,2,0:T(2,128)S(1)} %bitcast.59), channel_id=2, replica_groups=mesh['win'=4,'slab'=8] {'slab'}, dimensions={0}, use_global_device_ids=true | all-gather | bytes 288 | tf_op jit(solution)/shard_map/all_gather | solution.py:352
  198.0 1.5 collective-permute-start.1
  200.0 1.1 collective-permute-done.1
  (31 shorter events, 6.2 us)
Async XLA Ops:
  4.2 7.5 %collective-permute-start = (f32[4,32,512]{2,1,0:T(8,128)S(1)}, f32[4,32,512]{2,1,0:T(8,128)S(1)}, u32[]{:S(2)}, u32[]{:S(2)}) collective-permute-start(f32[4,32,512]{2,1,0:T(8,128)S(1)} %concatenate.6), channel_id=1, source_target_pairs={{0,1},{1,2},{2,3},{3,4},{4,5},{5,6},{6,7},{7,0},{8,9},{9,10},{10,1... | collective-permute-start | bytes 786440 | tf_op jit(solution)/shard_map/ppermute | solution.py:26
  34.7 30.2 %all-to-all-start = ((f32[8,2,256,128]{3,2,1,0:T(8,128)}), f32[8,2,256,128]{3,2,1,0:T(8,128)S(1)}, u32[]{:S(2)}, u32[]{:S(2)}) async-start(f32[8,2,256,128]{3,2,1,0:T(8,128)} %shard_map.139), calls=%async_computation | async-start | bytes 4194304 | tf_op jit(solution)/shard_map/all_to_all | solution.py:316
  64.9 1.4 copy-start.1
  66.2 30.2 %all-to-all-start.2 = ((f32[8,2,256,128]{3,2,1,0:T(8,128)}), f32[8,2,256,128]{3,2,1,0:T(8,128)S(1)}, u32[]{:S(2)}, u32[]{:S(2)}) async-start(f32[8,2,256,128]{3,2,1,0:T(8,128)} %shard_map.142), calls=%async_computation.2 | async-start | bytes 4194304 | tf_op jit(solution)/shard_map/all_to_all | solution.py:316
  96.4 1.4 copy-start
  97.8 31.0 %all-to-all-start.1 = ((f32[8,2,256,128]{3,2,1,0:T(8,128)}), f32[8,2,256,128]{3,2,1,0:T(8,128)}, u32[]{:S(2)}, u32[]{:S(2)}) async-start(f32[8,2,256,128]{3,2,1,0:T(8,128)} %shard_map.140), calls=%async_computation.1 | async-start | bytes 4194304 | tf_op jit(solution)/shard_map/all_to_all | solution.py:322
  128.8 30.4 %all-to-all-start.3 = ((f32[8,2,256,128]{3,2,1,0:T(8,128)}), f32[8,2,256,128]{3,2,1,0:T(8,128)S(1)}, u32[]{:S(2)}, u32[]{:S(2)}) async-start(f32[8,2,256,128]{3,2,1,0:T(8,128)} %shard_map.143), calls=%async_computation.3 | async-start | bytes 4194304 | tf_op jit(solution)/shard_map/all_to_all | solution.py:322
  159.1 27.9 %copy-start.3 = (f32[2,2,8,512]{3,2,1,0:T(8,128)S(1)}, f32[2,2,8,512]{3,2,1,0:T(8,128)}, u32[]{:S(2)}) copy-start(f32[2,2,8,512]{3,2,1,0:T(8,128)} %shard_map.141) | copy-start | bytes 196612
  159.1 1.3 copy-start.2
  198.0 3.1 %collective-permute-start.1 = (f32[4,3,512]{2,1,0:T(4,128)S(1)}, f32[4,3,512]{2,1,0:T(4,128)S(1)}, u32[]{:S(2)}, u32[]{:S(2)}) collective-permute-start(f32[4,3,512]{2,1,0:T(4,128)S(1)} %maximum_bitcast_fusion), channel_id=1, source_target_pairs={{0,7},{1,0},{2,1},{3,2},{4,3},{5,4},{6,5},{7,6},{8,15},{9,8},{10,9... | collective-permute-start | bytes 73736 | tf_op jit(solution)/shard_map/ppermute | solution.py:26

commit v2 on v1

--- a/solution.py
+++ b/solution.py
@@ -17,7 +17,7 @@
 
 CHARGE, STEP, CELL_X, CELL_Y, CELL_Z = 0, 1, 2, 3, 4
 WX, WY, WZ, SX, SY, SZ = 8, 12, 16, 20, 24, 28
-ROWS = 32
+BATCH = 4
 
 
 def passed_along(value, axis, steps):
@@ -78,49 +78,83 @@
     return min(depth, depth + REACH - distance * depth)
 
 
+def planes_at_once(count):
+    return max(size for size in range(1, BATCH + 1) if count % size == 0)
+
+
 def spread_kernel(depth, columns, native, atoms_ref, ty_ref, tx_ref, out_ref, grid_ref):
     sets = atoms_ref.shape[0]
-    for part in range(2):
-        lanes = slice(part * NY, (part + 1) * NY)
+
+    def one_window(part, carry):
         for distance in range(sets):
             record = atoms_ref[distance, part]
             rows_x = stencil_rows(record, CELL_X, WX, NX)
-            rows_y = split(stencil_rows(record, CELL_Y, WY, NY))
+            rows_y = jnp.concatenate(split(stencil_rows(record, CELL_Y, WY, NY)), axis=0)
             charge = record[CHARGE : CHARGE + 1]
-
-            def one_plane(plane, carry):
-                strength = plane_row(record, WZ, plane, distance * depth) * charge
-                spread = dot3(split(rows_x * strength), rows_y, ((1,), (1,)))
-                if distance == 0:
-                    grid_ref[plane, :, lanes] = spread
-                else:
-                    grid_ref[plane, :, lanes] += spread
+            count = planes_reached(distance, depth)
+            size = planes_at_once(count)
+
+            def some_planes(step, carry):
+                high, low = [], []
+                for k in range(size):
+                    plane = step * size + k
+                    strength = plane_row(record, WZ, plane, distance * depth) * charge
+                    pair = split(rows_x * strength)
+                    high.append(pair[0])
+                    low.append(pair[1])
+                products = lax.dot_general(
+                    jnp.concatenate(high + low, axis=0),
+                    rows_y,
+                    (((1,), (1,)), ((), ())),
+                    preferred_element_type=jnp.float32,
+                )
+                for k in range(size):
+                    top, bottom = k * NX, (size + k) * NX
+                    spread = products[top : top + NX, :NY] + (
+                        products[top : top + NX, NY:] + products[bottom : bottom + NX, :NY]
+                    )
+                    if distance == 0:
+                        grid_ref[part, step * size + k] = spread
+                    else:
+                        grid_ref[part, step * size + k] += spread
                 return carry
 
-            lax.fori_loop(0, planes_reached(distance, depth), one_plane, 0)
-
+            lax.fori_loop(0, count // size, some_planes, 0)
+        return carry
+
+    lax.fori_loop(0, 2, one_window, 0)
     table_y = (ty_ref[0], ty_ref[1])
     table_x = (tx_ref[0], tx_ref[1])
-
-    def transform(plane, carry):
-        along_y = dot3(split(grid_ref[plane]), table_y)
-        real, imaginary = along_y[:, :NY], along_y[:, NY:]
-        stacked = jnp.concatenate(
-            [along_y, jnp.concatenate([imaginary, -real], axis=1)], axis=0
-        )
-        both = dot3(table_x, split(stacked))
-        for part in range(2):
-            lanes = slice(part * NY, (part + 1) * NY)
-            if native:
-                for owner in range(NX // columns):
-                    out_ref[owner, part, pl.ds(plane, columns, stride=depth), :] = both[
-                        owner * columns : (owner + 1) * columns, lanes
-                    ]
-            else:
-                out_ref[plane, part] = both[:, lanes]
+    size = planes_at_once(depth)
+
+    def transform(step, carry):
+        packed = [
+            jnp.concatenate(
+                [grid_ref[0, step * size + k], grid_ref[1, step * size + k]], axis=1
+            )
+            for k in range(size)
+        ]
+        rows = dot3(split(jnp.concatenate(packed, axis=0)), table_y)
+        for k in range(size):
+            plane = step * size + k
+            along_y = rows[k * NX : (k + 1) * NX]
+            real, imaginary = along_y[:, :NY], along_y[:, NY:]
+            stacked = jnp.concatenate(
+                [along_y, jnp.concatenate([imaginary, -real], axis=1)], axis=0
+            )
+            both = dot3(table_x, split(stacked))
+            for part in range(2):
+                lanes = slice(part * NY, (part + 1) * NY)
+                if native:
+                    for owner in range(NX // columns):
+                        out_ref[owner, part, pl.ds(plane, columns, stride=depth), :] = both[
+                            owner * columns : (owner + 1) * columns, lanes
+                        ]
+                else:
+                    out_ref[plane, part] = both[:, lanes]
         return carry
 
-    lax.fori_loop(0, depth, transform, 0)
+    lax.fori_loop(0, depth // size, transform, 0)
 
 
 def column_kernel(columns, in_ref, influence_ref, forward_ref, inverse_ref, out_ref):
@@ -162,63 +196,92 @@
 
 
 def sample_kernel(
-    depth, columns, native, in_ref, atoms_ref, ty_ref, tx_ref, out_ref, high_ref, low_ref, sums_ref
+    depth, columns, native, in_ref, atoms_ref, ty_ref, tx_ref, out_ref, values_ref, sums_ref
 ):
     sets = atoms_ref.shape[0]
     atoms = atoms_ref.shape[3]
     table_y = (ty_ref[0], ty_ref[1])
     table_x = (tx_ref[0], tx_ref[1])
-
-    def transform(plane, carry):
-        pieces = []
-        for part in range(2):
-            if native:
-                pieces.append(
-                    jnp.concatenate(
-                        [
-                            in_ref[owner, part, pl.ds(plane, columns, stride=depth), :]
-                            for owner in range(NX // columns)
-                        ],
-                        axis=0,
+    size = planes_at_once(depth)
+
+    def transform(step, carry):
+        rows = []
+        for k in range(size):
+            plane = step * size + k
+            pieces = []
+            for part in range(2):
+                if native:
+                    pieces.append(
+                        jnp.concatenate(
+                            [
+                                in_ref[owner, part, pl.ds(plane, columns, stride=depth), :]
+                                for owner in range(NX // columns)
+                            ],
+                            axis=0,
+                        )
                     )
-                )
-            else:
-                pieces.append(in_ref[plane, part])
-        real, imaginary = pieces
-        stacked = jnp.concatenate(
-            [
-                jnp.concatenate([real, imaginary], axis=1),
-                jnp.concatenate([-imaginary, real], axis=1),
-            ],
-            axis=0,
-        )
-        along_x = dot3(table_x, split(stacked))
-        high, low = split(dot3(split(along_x), table_y))
-        high_ref[plane] = high
-        low_ref[plane] = low
+                else:
+                    pieces.append(in_ref[plane, part])
+            real, imaginary = pieces
+            stacked = jnp.concatenate(
+                [
+                    jnp.concatenate([real, imaginary], axis=1),
+                    jnp.concatenate([-imaginary, real], axis=1),
+                ],
+                axis=0,
+            )
+            rows.append(dot3(table_x, split(stacked)))
+        high, low = split(dot3(split(jnp.concatenate(rows, axis=0)), table_y))
+        for k in range(size):
+            span = slice(k * NX, (k + 1) * NX)
+            for part in range(2):
+                lanes = slice(part * NY, (part + 1) * NY)
+                values_ref[part, step * size + k] = jnp.concatenate(
+                    [high[span, lanes], low[span, lanes]], axis=1
+                )
         return carry
 
-    lax.fori_loop(0, depth, transform, 0)
-
-    for part in range(2):
-        lanes = slice(part * NY, (part + 1) * NY)
+    lax.fori_loop(0, depth // size, transform, 0)
+
+    def one_window(part, carry):
         for distance in range(sets):
             record = atoms_ref[distance, part]
-            rows_y = split(stencil_rows(record, CELL_Y, WY, NY))
-            steep_y = split(stencil_rows(record, CELL_Y, SY, NY))
+            high_y, low_y = split(
+                jnp.concatenate(
+                    [
+                        stencil_rows(record, CELL_Y, WY, NY),
+                        stencil_rows(record, CELL_Y, SY, NY),
+                    ],
+                    axis=1,
+                )
+            )
+            both_y = jnp.concatenate([high_y, high_y], axis=0)
             sums_ref[...] = jnp.zeros(sums_ref.shape, jnp.float32)
-
-            def one_plane(plane, carry):
-                values = (high_ref[plane, :, lanes], low_ref[plane, :, lanes])
-                weight = plane_row(record, WZ, plane, distance * depth)
-                slope = plane_row(record, SZ, plane, distance * depth)
-                along = dot3(values, rows_y)
-                sums_ref[0] += weight * along
-                sums_ref[1] += slope * along
-                sums_ref[2] += weight * dot3(values, steep_y)
+            count = planes_reached(distance, depth)
+            size = planes_at_once(count)
+
+            def some_planes(step, carry):
+                first = step * size
+                values = jnp.concatenate(
+                    [values_ref[part, first + k] for k in range(size)], axis=0
+                )
+                along = jnp.dot(values, both_y, preferred_element_type=jnp.float32) + jnp.dot(
+                    values[:, :NY], low_y, preferred_element_type=jnp.float32
+                )
+                level, rise, across = sums_ref[0], sums_ref[1], sums_ref[2]
+                for k in range(size):
+                    weight = plane_row(record, WZ, first + k, distance * depth)
+                    slope = plane_row(record, SZ, first + k, distance * depth)
+                    plain = along[k * NX : (k + 1) * NX, :atoms]
+                    level += weight * plain
+                    rise += slope * plain
+                    across += weight * along[k * NX : (k + 1) * NX, atoms:]
+                sums_ref[0] = level
+                sums_ref[1] = rise
+                sums_ref[2] = across
                 return carry
 
-            lax.fori_loop(0, planes_reached(distance, depth), one_plane, 0)
+            lax.fori_loop(0, count // size, some_planes, 0)
             rows_x = stencil_rows(record, CELL_X, WX, NX)
             steep_x = stencil_rows(record, CELL_X, SX, NX)
             charge = record[CHARGE : CHARGE + 1]
@@ -237,6 +300,9 @@
                 ],
                 axis=0,
             )
+        return carry
+
+    lax.fori_loop(0, 2, one_window, 0)
 
 
 def influence_block(first_column, column_count):
@@ -329,7 +395,7 @@
         planes = call(
             functools.partial(spread_kernel, depth, columns, native),
             slab_shape,
-            [pltpu.VMEM((depth, NX, 2 * NY), jnp.float32)],
+            [pltpu.VMEM((2, depth, NX, NY), jnp.float32)],
         )(mine, forward_y, table_x)
         back = call(functools.partial(column_kernel, columns), column_shape)(
             to_columns(planes), influence, forward_z, inverse_z
@@ -339,8 +405,7 @@
                 functools.partial(sample_kernel, depth, columns, native),
                 (reach + 1, 2, 8, atoms),
                 [
-                    pltpu.VMEM((depth, NX, 2 * NY), jnp.bfloat16),
-                    pltpu.VMEM((depth, NX, 2 * NY), jnp.bfloat16),
+                    pltpu.VMEM((2, depth, NX, 2 * NY), jnp.bfloat16),
                     pltpu.VMEM((3, NX, atoms), jnp.float32),
                 ],
             )(to_planes(back), mine, inverse_y, table_x)
@@ -349,7 +414,8 @@
     partial_sums = jnp.sum(
         results[:, :, :1] * records[:, :windows, CHARGE : STEP + 1], axis=(0, 3)
     )
-    sums = jnp.sum(lax.all_gather(partial_sums, "slab"), axis=0)
+    copies = jnp.broadcast_to(partial_sums[None], (slabs,) + partial_sums.shape)
+    sums = jnp.sum(lax.all_to_all(copies, "slab", 0, 0, tiled=True), axis=0)
     forces = results[0, :, 1:4]
     for distance in range(1, reach + 1):
         forces = forces + passed_along(results[distance, :, 1:4], "slab", -distance)

time: 204 us -> 177 us (0.87)
  Pallas kernels: 115 us -> 70 us
  waiting for transfers between devices: 46.5 us -> 69 us
  blocking collectives: 9.16 us -> 0 us
  starting transfers between devices: 17.3 us -> 21.8 us
    pallas_call x2, Pallas kernels: 53.1 us -> 27.7 us  [body(): call(functools.partial(sample_kernel, depth, columns, native), (reach + 1...]
    pallas_call x2, Pallas kernels: 44.4 us -> 24.8 us  [body(): call(functools.partial(spread_kernel, depth, columns, native), slab_shape...]
    all_to_all x2, waiting for transfers between devices: 17.9 us -> 30.4 us  [to_planes(): return lax.all_to_all(value, 'slab', 0, 0, tiled=True)]
    all_to_all x2, waiting for transfers between devices: 20.6 us -> 30.4 us  [to_columns(): return lax.all_to_all(value, 'slab', 0, 0, tiled=True)]
    all_gather x1 -> x0, blocking collectives: 9.16 us -> none  [body(): sums = jnp.sum(lax.all_gather(partial_sums, 'slab'), axis=0)]
    all_to_all x0 -> x1, starting transfers between devices: none -> 3.33 us  [body(): sums = jnp.sum(lax.all_to_all(copies, 'slab', 0, 0, tiled=True), axis=0)]
  transfers between devices with their start and end apart: 6 -> 7, of which waited for: 5 -> 6; matrix products, arithmetic and copies ran while one was open for 1% -> 2% of each run, Pallas kernels for 33% -> 25%
where the time goes in v2:
time: 177 us; the launch traced here: 176 us
  Pallas kernels  70 us (40%)
  waiting for transfers between devices  69 us (39%)
  starting transfers between devices  21.8 us (12%)
  local copies, waits for them, and re-layouts  7.27 us (4%)
  other arithmetic  7.05 us (4%)
    all_to_all x2, waiting for transfers between devices, to_planes(): return lax.all_to_all(value, 'slab', 0, 0, tiled=True)  30.4 us
    all_to_all x2, waiting for transfers between devices, to_columns(): return lax.all_to_all(value, 'slab', 0, 0, tiled=True)  30.4 us
    pallas_call x2, Pallas kernels, body(): call(functools.partial(sample_kernel, depth, columns, native), (reach + 1...  27.7 us
    pallas_call x2, Pallas kernels, body(): call(functools.partial(spread_kernel, depth, columns, native), slab_shape...  24.8 us
    pallas_call x2, Pallas kernels, body(): call(functools.partial(column_kernel, columns), column_shape)  17.5 us
    all_to_all x2, starting transfers between devices, to_planes(): return lax.all_to_all(value, 'slab', 0, 0, tiled=True)  8.12 us
    all_to_all x2, starting transfers between devices, to_columns(): return lax.all_to_all(value, 'slab', 0, 0, tiled=True)  7.2 us
    ppermute x2, waiting for transfers between devices, passed_along(): return lax.ppermute(value, axis, pairs)  6.93 us
  transfers between devices with their start and end apart: 7, of which 6 were waited for; matrix products, arithmetic and copies ran while one was open for 2% of the time, Pallas kernels for 25%

profile of v2, /device:TPU:0, one launch (start us, length us, event | category | flops | bytes accessed | tf_op | source)
XLA Modules:
  0.0 175.9 jit_solution(2131663179513076247)
XLA Ops:
  4.7 6.9 %collective-permute-done = f32[4,32,512]{2,1,0:T(8,128)S(1)} collective-permute-done((f32[4,32,512]{2,1,0:T(8,128)S(1)}, f32[4,32,512]{2,1,0:T(8,128)S(1)}, u32[]{:S(2)}, u32[]{:S(2)}) %collective-permute-start) | collective-permute-done | bytes 262176 | tf_op jit(solution)/shard_map/ppermute | solution.py:26
  11.6 0.9 fusion.5
  12.5 12.4 %shard_map.139 = f32[8,2,256,128]{3,2,1,0:T(8,128)} custom-call(f32[2,2,32,512]{3,2,1,0:T(8,128)} %get-tuple-element.12.atoms_ref, bf16[2,256,256]{2,1,0:T(8,128)(2,1)} %constant.43.clone.ty_ref.inverse_ref, bf16[2,128,256]{2,1,0:T(8,128)(2,1)} %constant.42.clone.tx_ref), custom_call_target="tpu_custom_call" | custom-call | flops 8000000000 | bytes 4000000 | tf_op jit(solution)/shard_map/pallas_call | solution.py:395
  24.9 3.6 %all-to-all-start = ((f32[8,2,256,128]{3,2,1,0:T(8,128)}), f32[8,2,256,128]{3,2,1,0:T(8,128)S(1)}, u32[]{:S(2)}, u32[]{:S(2)}) async-start(f32[8,2,256,128]{3,2,1,0:T(8,128)} %shard_map.139), calls=%async_computation | async-start | bytes 4194304 | tf_op jit(solution)/shard_map/all_to_all | solution.py:382
  28.5 12.4 %shard_map.142 = f32[8,2,256,128]{3,2,1,0:T(8,128)} custom-call(f32[2,2,32,512]{3,2,1,0:T(8,128)} %get-tuple-element.13.atoms_ref, bf16[2,256,256]{2,1,0:T(8,128)(2,1)} %constant.43.clone.ty_ref.inverse_ref, bf16[2,128,256]{2,1,0:T(8,128)(2,1)} %constant.42.clone.tx_ref), custom_call_target="tpu_custom_call" | custom-call | flops 8000000000 | bytes 4000000 | tf_op jit(solution)/shard_map/pallas_call | solution.py:395
  40.9 14.2 %all-to-all-done.in_ref = f32[8,2,256,128]{3,2,1,0:T(8,128)S(1)} async-done(((f32[8,2,256,128]{3,2,1,0:T(8,128)}), f32[8,2,256,128]{3,2,1,0:T(8,128)S(1)}, u32[]{:S(2)}, u32[]{:S(2)}) %all-to-all-start) | async-done | bytes 2097184 | tf_op jit(solution)/shard_map/all_to_all | solution.py:382
  55.1 1.4 copy-done.1
  56.5 3.6 %all-to-all-start.2 = ((f32[8,2,256,128]{3,2,1,0:T(8,128)}), f32[8,2,256,128]{3,2,1,0:T(8,128)S(1)}, u32[]{:S(2)}, u32[]{:S(2)}) async-start(f32[8,2,256,128]{3,2,1,0:T(8,128)} %shard_map.142), calls=%async_computation.2 | async-start | bytes 4194304 | tf_op jit(solution)/shard_map/all_to_all | solution.py:382
  60.2 1.5 fusion.influence_ref
  61.7 8.8 %shard_map.140 = f32[8,2,256,128]{3,2,1,0:T(8,128)} custom-call(f32[8,2,256,128]{3,2,1,0:T(8,128)} %copy-done.1, f32[16,128,128]{2,1,0:T(8,128)} %fusion.influence_ref, bf16[2,256,256]{2,1,0:T(8,128)(2,1)} %constant.44.clone.forward_ref.ty_ref, bf16[2,256,256]{2,1,0:T(8,128)(2,1)} %constant.43.clone.ty_ref.inverse_ref), custom_call_target="tpu_custom_call" | custom-call | flops 8000000000 | bytes 4000000 | tf_op jit(solution)/shard_map/pallas_call | solution.py:400
  70.4 16.2 %all-to-all-done.2.in_ref = f32[8,2,256,128]{3,2,1,0:T(8,128)S(1)} async-done(((f32[8,2,256,128]{3,2,1,0:T(8,128)}), f32[8,2,256,128]{3,2,1,0:T(8,128)S(1)}, u32[]{:S(2)}, u32[]{:S(2)}) %all-to-all-start.2) | async-done | bytes 2097184 | tf_op jit(solution)/shard_map/all_to_all | solution.py:382
  86.6 1.4 copy-done
  88.0 4.3 %all-to-all-start.1 = ((f32[8,2,256,128]{3,2,1,0:T(8,128)}), f32[8,2,256,128]{3,2,1,0:T(8,128)}, u32[]{:S(2)}, u32[]{:S(2)}) async-start(f32[8,2,256,128]{3,2,1,0:T(8,128)} %shard_map.140), calls=%async_computation.1 | async-start | bytes 4194304 | tf_op jit(solution)/shard_map/all_to_all | solution.py:388
  92.3 8.8 %shard_map.143 = f32[8,2,256,128]{3,2,1,0:T(8,128)} custom-call(f32[8,2,256,128]{3,2,1,0:T(8,128)} %copy-done, f32[16,128,128]{2,1,0:T(8,128)} %fusion.influence_ref, bf16[2,256,256]{2,1,0:T(8,128)(2,1)} %constant.44.clone.forward_ref.ty_ref, bf16[2,256,256]{2,1,0:T(8,128)(2,1)} %constant.43.clone.ty_ref.inverse_ref), custom_call_target="tpu_custom_call" | custom-call | flops 8000000000 | bytes 4000000 | tf_op jit(solution)/shard_map/pallas_call | solution.py:400
  101.1 17.9 %all-to-all-done.1.in_ref = f32[8,2,256,128]{3,2,1,0:T(8,128)} async-done(((f32[8,2,256,128]{3,2,1,0:T(8,128)}), f32[8,2,256,128]{3,2,1,0:T(8,128)}, u32[]{:S(2)}, u32[]{:S(2)}) %all-to-all-start.1) | async-done | bytes 2097184 | tf_op jit(solution)/shard_map/all_to_all | solution.py:388
  118.9 3.8 %all-to-all-start.3 = ((f32[8,2,256,128]{3,2,1,0:T(8,128)}), f32[8,2,256,128]{3,2,1,0:T(8,128)S(1)}, u32[]{:S(2)}, u32[]{:S(2)}) async-start(f32[8,2,256,128]{3,2,1,0:T(8,128)} %shard_map.143), calls=%async_computation.3 | async-start | bytes 4194304 | tf_op jit(solution)/shard_map/all_to_all | solution.py:388
  122.7 13.9 %shard_map.141 = f32[2,2,8,512]{3,2,1,0:T(8,128)} custom-call(f32[8,2,256,128]{3,2,1,0:T(8,128)} %all-to-all-done.1.in_ref, f32[2,2,32,512]{3,2,1,0:T(8,128)} %get-tuple-element.12.atoms_ref, bf16[2,256,256]{2,1,0:T(8,128)(2,1)} %constant.44.clone.forward_ref.ty_ref, bf16[2,128,256]{2,1,0:T(8,128)(2,1)} %constant.42.clone.tx_ref), custom_call_target="tpu_custom_call" | custom-call | flops 8000000000 | bytes 4000000 | tf_op jit(solution)/shard_map/pallas_call | solution.py:404
  136.6 12.5 %all-to-all-done.3.in_ref = f32[8,2,256,128]{3,2,1,0:T(8,128)S(1)} async-done(((f32[8,2,256,128]{3,2,1,0:T(8,128)}), f32[8,2,256,128]{3,2,1,0:T(8,128)S(1)}, u32[]{:S(2)}, u32[]{:S(2)}) %all-to-all-start.3) | async-done | bytes 2097184 | tf_op jit(solution)/shard_map/all_to_all | solution.py:388
  149.1 1.3 copy-done.2
  150.4 13.8 %shard_map.144 = f32[2,2,8,512]{3,2,1,0:T(8,128)} custom-call(f32[8,2,256,128]{3,2,1,0:T(8,128)} %copy-done.2, f32[2,2,32,512]{3,2,1,0:T(8,128)} %get-tuple-element.13.atoms_ref, bf16[2,256,256]{2,1,0:T(8,128)(2,1)} %constant.44.clone.forward_ref.ty_ref, bf16[2,128,256]{2,1,0:T(8,128)(2,1)} %constant.42.clone.tx_ref), custom_call_target="tpu_custom_call" | custom-call | flops 8000000000 | bytes 4000000 | tf_op jit(solution)/shard_map/pallas_call | solution.py:404
  164.3 0.8 pad_maximum_fusion.1
  166.0 3.3 %all-to-all-start.4 = ((f32[8,4,2]{1,2,0:T(2,128)}), f32[8,4,2]{1,2,0:T(2,128)S(1)}, u32[]{:S(2)}, u32[]{:S(2)}) async-start(f32[8,4,2]{1,2,0:T(2,128)} %broadcast_in_dim.28), calls=%async_computation.4 | async-start | bytes 16384 | tf_op jit(solution)/shard_map/all_to_all | solution.py:418
  170.1 2.6 %collective-permute-start.1 = (f32[4,3,512]{2,1,0:T(4,128)S(1)}, f32[4,3,512]{2,1,0:T(4,128)S(1)}, u32[]{:S(2)}, u32[]{:S(2)}) collective-permute-start(f32[4,3,512]{2,1,0:T(4,128)S(1)} %maximum_bitcast_fusion), channel_id=1, source_target_pairs={{0,7},{1,0},{2,1},{3,2},{4,3},{5,4},{6,5},{7,6},{8,15},{9,8},{10,9... | collective-permute-start | bytes 73736 | tf_op jit(solution)/shard_map/ppermute | solution.py:26
  172.6 1.3 all-to-all-done.4
  (33 shorter events, 7.6 us)
Async XLA Ops:
  4.2 7.5 %collective-permute-start = (f32[4,32,512]{2,1,0:T(8,128)S(1)}, f32[4,32,512]{2,1,0:T(8,128)S(1)}, u32[]{:S(2)}, u32[]{:S(2)}) collective-permute-start(f32[4,32,512]{2,1,0:T(8,128)S(1)} %concatenate.6), channel_id=1, source_target_pairs={{0,1},{1,2},{2,3},{3,4},{4,5},{5,6},{6,7},{7,0},{8,9},{9,10},{10,1... | collective-permute-start | bytes 786440 | tf_op jit(solution)/shard_map/ppermute | solution.py:26
  24.9 30.2 %all-to-all-start = ((f32[8,2,256,128]{3,2,1,0:T(8,128)}), f32[8,2,256,128]{3,2,1,0:T(8,128)S(1)}, u32[]{:S(2)}, u32[]{:S(2)}) async-start(f32[8,2,256,128]{3,2,1,0:T(8,128)} %shard_map.139), calls=%async_computation | async-start | bytes 4194304 | tf_op jit(solution)/shard_map/all_to_all | solution.py:382
  55.1 1.4 copy-start.1
  56.5 30.2 %all-to-all-start.2 = ((f32[8,2,256,128]{3,2,1,0:T(8,128)}), f32[8,2,256,128]{3,2,1,0:T(8,128)S(1)}, u32[]{:S(2)}, u32[]{:S(2)}) async-start(f32[8,2,256,128]{3,2,1,0:T(8,128)} %shard_map.142), calls=%async_computation.2 | async-start | bytes 4194304 | tf_op jit(solution)/shard_map/all_to_all | solution.py:382
  86.6 1.4 copy-start
  88.0 31.0 %all-to-all-start.1 = ((f32[8,2,256,128]{3,2,1,0:T(8,128)}), f32[8,2,256,128]{3,2,1,0:T(8,128)}, u32[]{:S(2)}, u32[]{:S(2)}) async-start(f32[8,2,256,128]{3,2,1,0:T(8,128)} %shard_map.140), calls=%async_computation.1 | async-start | bytes 4194304 | tf_op jit(solution)/shard_map/all_to_all | solution.py:388
  118.9 30.2 %all-to-all-start.3 = ((f32[8,2,256,128]{3,2,1,0:T(8,128)}), f32[8,2,256,128]{3,2,1,0:T(8,128)S(1)}, u32[]{:S(2)}, u32[]{:S(2)}) async-start(f32[8,2,256,128]{3,2,1,0:T(8,128)} %shard_map.143), calls=%async_computation.3 | async-start | bytes 4194304 | tf_op jit(solution)/shard_map/all_to_all | solution.py:388
  136.6 27.7 %copy-start.3 = (f32[2,2,8,512]{3,2,1,0:T(8,128)S(1)}, f32[2,2,8,512]{3,2,1,0:T(8,128)}, u32[]{:S(2)}) copy-start(f32[2,2,8,512]{3,2,1,0:T(8,128)} %shard_map.141) | copy-start | bytes 196612
  149.1 1.3 copy-start.2
  166.0 8.0 %all-to-all-start.4 = ((f32[8,4,2]{1,2,0:T(2,128)}), f32[8,4,2]{1,2,0:T(2,128)S(1)}, u32[]{:S(2)}, u32[]{:S(2)}) async-start(f32[8,4,2]{1,2,0:T(2,128)} %broadcast_in_dim.28), calls=%async_computation.4 | async-start | bytes 16384 | tf_op jit(solution)/shard_map/all_to_all | solution.py:418
  170.1 4.4 %collective-permute-start.1 = (f32[4,3,512]{2,1,0:T(4,128)S(1)}, f32[4,3,512]{2,1,0:T(4,128)S(1)}, u32[]{:S(2)}, u32[]{:S(2)}) collective-permute-start(f32[4,3,512]{2,1,0:T(4,128)S(1)} %maximum_bitcast_fusion), channel_id=1, source_target_pairs={{0,7},{1,0},{2,1},{3,2},{4,3},{5,4},{6,5},{7,6},{8,15},{9,8},{10,9... | collective-permute-start | bytes 73736 | tf_op jit(solution)/shard_map/ppermute | solution.py:26
